TPU v7x, 32 devices: a whole 2x2x4 slice. The times are simulated.
32 devices in a mesh: row: 4 (over z), col: 4 (over x, core), layer: 2 (over y).
Axes of the slice: x: 2, y: 2, z: 4, core: 2. Of those that a mesh axis runs over, the one named last changes fastest.
Arguments:
- left: bfloat16 [4096, 8192], P('row', ('col', 'layer')), may hold values from -6 to 6
- middle: bfloat16 [8192, 8192], P('row', 'col'), may hold values from -0.0625 to 0.0625
- right: bfloat16 [8192, 8192], P('row', 'col'), may hold values from -0.0625 to 0.0625
Outputs:
- product: bfloat16 [4096, 8192], P('row', ('col', 'layer'))
All inputs are finite; a program needn't handle non-finite values.
Results may differ from a plain program's by a relative error of at most 0.0049.
Values may be sent and summed in bfloat16 or wider, within the bound.
A program may use at most 128 MiB of HBM per device.

v0:
```python
import functools

import jax
import jax.numpy as jnp
from jax import lax
from jax.experimental import pallas as pl
from jax.experimental.pallas import tpu as pltpu
from jax.sharding import PartitionSpec as P

CHUNKS = 4
TILE = 256
MESH = pl.DeviceIdType.MESH


def kernel(
    rows, cols, layers,
    left_ref, middle_ref, right_ref, out_ref,
    held, held2, rhs, sent, kept, near, far, near2,
    own_sem, home_sem, swap_sems, pair_sems, plane_sems, core_sems, near_sems, far_sems, near2_sems, hop_sems, relay_sems,
):
    group, side = rows // 2, cols // 2
    row, col, layer = lax.axis_index("row"), lax.axis_index("col"), lax.axis_index("layer")
    h, z = row // group, lax.rem(row, group)
    x, c = col // side, lax.rem(col, side)
    straight = h == x
    depth = middle_ref.shape[0]
    width = out_ref.shape[1]
    inner = left_ref.shape[1]
    chunk = left_ref.shape[0] // CHUNKS
    tile = min(TILE, width)

    def at(h_, x_):
        return (h_ * group + z, x_ * side + c, layer)

    def slot(col_, layer_):
        return col_ * layers + layer_

    sibling = col + 1 - 2 * lax.rem(col, 2)
    offsets = [(dc, dl) for dc in range(cols // 2) for dl in range(layers) if dc or dl]

    def moved(col_, dc, dl, sign):
        return lax.rem(col_ + sign * 2 * dc + cols, cols), lax.rem(layer + sign * dl + layers, layers)

    barrier = pltpu.get_barrier_semaphore()
    greeted = [at(1 - h, x), at(h, 1 - x), at(1 - h, 1 - x), (row, sibling, layer)]
    for shift in range(1, group):
        greeted.append((h * group + lax.rem(z + shift, group), col, layer))
    for dc, dl in offsets:
        greeted.append((row, *moved(col, dc, dl, 1)))
    for device in greeted:
        pl.semaphore_signal(barrier, inc=1, device_id=device, device_id_type=MESH)
    pl.semaphore_wait(barrier, len(greeted))

    me = slot(col, layer)

    def part(j):
        return pl.ds(j * chunk, chunk)

    def remote(src, dst, sems, device):
        return pltpu.make_async_remote_copy(
            src_ref=src, dst_ref=dst, send_sem=sems.at[0], recv_sem=sems.at[1],
            device_id=device, device_id_type=MESH,
        )

    home = pltpu.make_async_copy(left_ref, held.at[me], home_sem)

    def swap(j):
        device = at(1 - h, x) if j % 2 else at(h, 1 - x)
        return remote(left_ref.at[part(j)], near2.at[part(j)], swap_sems.at[j], device)

    def hop(j):
        device = at(h, 1 - x) if j % 2 else at(1 - h, x)
        target = slot((1 - x) * side + c, layer) if j % 2 else me
        return remote(near2.at[part(j)], held.at[target, part(j)], hop_sems.at[j], device)

    columns = pl.ds(pl.multiple_of(layer * width, width), width)
    pieces = CHUNKS
    step = depth // pieces

    def own(which):
        ref = (middle_ref, right_ref)[which]
        return pltpu.make_async_copy(
            ref.at[:, columns], rhs.at[which, pl.ds(z * depth, depth)], own_sem.at[which]
        )

    def pair(which, piece, shift):
        ref = (middle_ref, right_ref)[which]
        return remote(
            ref.at[pl.ds(piece * step, step), columns],
            rhs.at[which, pl.ds(z * depth + piece * step, step)],
            pair_sems.at[which, piece, shift - 1],
            (h * group + lax.rem(z + shift, group), col, layer),
        )

    def pair_start(which, piece):
        for shift in range(1, group):
            pair(which, piece, shift).start()

    def pair_wait(which):
        for piece in range(pieces):
            for shift in range(1, group):
                pair(which, piece, shift).wait_recv()
        own(which).wait()

    buffers = (held, held2)

    def spread(phase, j, index):
        dc, dl = offsets[index]
        ref = buffers[phase].at[me, part(j)]
        return remote(ref, ref, plane_sems.at[phase, j, index], (row, *moved(col, dc, dl, 1)))

    def pass_on(phase, j, index):
        origin = me
        if index:
            dc, dl = offsets[index - 1]
            origin = slot(*moved(col, dc, dl, -1))
        ref = buffers[phase].at[origin, part(j)]
        return remote(ref, ref, core_sems.at[phase, j, index], (row, sibling, layer))

    def spread_start(phase, j):
        for index in range(len(offsets)):
            spread(phase, j, index).start()
        pass_on(phase, j, 0).start()

    def spread_finish(phase, j):
        for index in range(len(offsets)):
            spread(phase, j, index).wait_recv()
            pass_on(phase, j, index + 1).start()
        for index in range(len(offsets) + 1):
            pass_on(phase, j, index).wait_recv()

    def multiply(phase, j, piece, target):
        blocks = side * layers
        ref = buffers[phase]

        @pl.loop(0, width // tile)
        def _(n):
            across = pl.ds(pl.multiple_of(n * tile, tile), tile)
            total = jnp.zeros((chunk, tile), jnp.float32)
            for k in range(blocks):
                total += jnp.dot(
                    ref[piece * blocks + k, part(j), :],
                    rhs[phase, pl.ds(k * inner, inner), across],
                    preferred_element_type=jnp.float32,
                )
            target[part(j), across] = total.astype(target.dtype)

    def add(one, two, j, store):
        @pl.loop(0, chunk // 32)
        def _(i):
            span = pl.ds(pl.multiple_of(j * chunk + i * 32, 32), 32)
            value = one[span, :].astype(jnp.float32) + two[span, :].astype(jnp.float32)
            store(span, value.astype(jnp.bfloat16))

    def near_copy(j):
        target_row = jnp.where(straight, h, x)
        target_col = jnp.where(straight, 1 - x, x)
        return remote(sent.at[part(j)], near.at[part(j)], near_sems.at[j], at(target_row, target_col))

    def far_copy(j):
        return remote(kept.at[part(j)], far.at[part(j)], far_sems.at[j], at(h, 1 - x))

    def relay_copy(j):
        return remote(far.at[part(j)], far.at[part(j)], relay_sems.at[j], at(1 - h, x))

    def near2_copy(j):
        return remote(sent.at[part(j)], near2.at[part(j)], near2_sems.at[j], at(1 - h, x))

    @pl.when(straight)
    def _():
        home.start()

    @pl.when(jnp.logical_not(straight))
    def _():
        for j in range(CHUNKS):
            swap(j).start()

    own(0).start()
    own(1).start()
    for piece in range(pieces):
        pair_start(0, piece)

    @pl.when(straight)
    def _():
        home.wait()

    for j in range(CHUNKS):
        @pl.when(straight)
        def _():
            swap(j).wait_recv()
            hop(j).start()

        @pl.when(jnp.logical_not(straight))
        def _():
            hop(j).wait_recv()

        spread_start(0, j)

    @pl.when(straight)
    def _():
        for j in range(CHUNKS):
            hop(j).wait_send()

    def first_done(j):
        near_copy(j).wait_recv()

        def store(span, value):
            held2[me, span, :] = value

        @pl.when(straight)
        def _():
            add(near, kept, j, store)

        @pl.when(jnp.logical_not(straight))
        def _():
            relay_copy(j).wait_recv()
            add(near, far, j, store)

        spread_start(1, j)

    for j in range(CHUNKS):
        spread_finish(0, j)
        if j == 0:
            pair_wait(0)
        multiply(0, j, h, kept)

        @pl.when(jnp.logical_not(straight))
        def _():
            far_copy(j).start()

        multiply(0, j, 1 - h, sent)
        near_copy(j).start()

        @pl.when(straight)
        def _():
            far_copy(j).wait_recv()
            relay_copy(j).start()

        pair_start(1, j)
        if j:
            first_done(j - 1)
    first_done(CHUNKS - 1)

    def out_done(j):
        near2_copy(j).wait_recv()

        def store(span, value):
            out_ref[span, :] = value

        add(near2, kept, j, store)

    for j in range(CHUNKS):
        spread_finish(1, j)
        if j == 0:
            pair_wait(1)
        near_copy(j).wait_send()

        @pl.when(jnp.logical_not(straight))
        def _():
            far_copy(j).wait_send()

        multiply(1, j, 1 - h, sent)
        near2_copy(j).start()
        multiply(1, j, h, kept)
        if j:
            out_done(j - 1)
    out_done(CHUNKS - 1)

    @pl.when(jnp.logical_not(straight))
    def _():
        for j in range(CHUNKS):
            swap(j).wait_send()

    @pl.when(straight)
    def _():
        for j in range(CHUNKS):
            relay_copy(j).wait_send()

    for j in range(CHUNKS):
        near2_copy(j).wait_send()
        for phase in range(2):
            for index in range(len(offsets)):
                spread(phase, j, index).wait_send()
            for index in range(len(offsets) + 1):
                pass_on(phase, j, index).wait_send()
    for which in range(2):
        for piece in range(pieces):
            for shift in range(1, group):
                pair(which, piece, shift).wait_send()


def per_device(left, middle, right):
    rows, cols, layers = (lax.axis_size(name) for name in ("row", "col", "layer"))
    height, inner = left.shape
    width = right.shape[1] // layers
    depth = right.shape[0]
    group = rows // 2
    partners = cols // 2 * layers - 1
    bf16 = jnp.bfloat16
    anywhere = pl.BlockSpec(memory_space=pl.ANY)
    dma = pltpu.SemaphoreType.DMA
    return pl.pallas_call(
        functools.partial(kernel, rows, cols, layers),
        out_shape=jax.ShapeDtypeStruct((height, width), bf16),
        in_specs=[anywhere] * 3,
        out_specs=pl.BlockSpec(memory_space=pltpu.VMEM),
        scratch_shapes=[
            pltpu.VMEM((cols * layers, height, inner), bf16),
            pltpu.VMEM((cols * layers, height, inner), bf16),
            pltpu.VMEM((2, group * depth, width), bf16),
        ]
        + [pltpu.VMEM((height, width), bf16)] * 5
        + [
            dma((2,)),
            dma,
            dma((CHUNKS, 2)),
            dma((2, CHUNKS, max(group - 1, 1), 2)),
            dma((2, CHUNKS, partners, 2)),
            dma((2, CHUNKS, partners + 1, 2)),
            dma((CHUNKS, 2)),
            dma((CHUNKS, 2)),
            dma((CHUNKS, 2)),
            dma((CHUNKS, 2)),
            dma((CHUNKS, 2)),
        ],
        compiler_params=pltpu.CompilerParams(
            collective_id=0, has_side_effects=True, vmem_limit_bytes=67043328
        ),
    )(left, middle, right)


def solution(mesh):
    return jax.shard_map(
        per_device,
        mesh=mesh,
        in_specs=(P("row", ("col", "layer")), P("row", "col"), P("row", "col")),
        out_specs=P("row", ("col", "layer")),
        check_vma=False,
    )
```

profile of v0, /device:TPU:14, one launch (start us, length us, event | category | flops | bytes accessed | tf_op | source)
XLA Modules:
  0.0 402.7 jit_solution(3065974293644803910)
XLA Ops:
  0.0 399.6 %shard_map.37 = bf16[1024,1024]{1,0:T(8,128)(2,1)} custom-call(bf16[1024,1024]{1,0:T(8,128)(2,1)} %left_ref.1, bf16[2048,2048]{1,0:T(8,128)(2,1)} %middle_ref.1, bf16[2048,2048]{1,0:T(8,128)(2,1)} %right_ref.1), custom_call_target="tpu_custom_call" | custom-call | tf_op jit(solution)/shard_map/pallas_call | solution.py:302
  399.6 3.1 copy.5
where the time goes:
time: 409 us; the launch traced here: 403 us
  Pallas kernels  400 us (98%)
    pallas_call x1, Pallas kernels, per_device(): pl.pallas_call(functools.partial(kernel, rows, cols, layers), out_shape=j...  400 us

commit v1 on v0

--- a/solution.py
+++ b/solution.py
@@ -9,6 +9,44 @@
 
 CHUNKS = 4
 TILE = 256
+PAIR = 2
+PIECES = 8
+INNER = (
+    (0,), (1,), (2, 1), (2, 0), (4, 0, 0), (4, 0, 1), (4, 0, 2), (4, 0, 3), (6, 0, 0), (4, 0, 4), (4, 0, 5),
+    (4, 0, 6), (5, 0), (9, 0), (6, 0, 1), (10, 1), (16, 0, 1), (4, 0, 7), (3, 0), (6, 0, 2), (6, 0, 3), (10, 0),
+    (3, 1), (5, 1), (6, 0, 4), (16, 0, 0), (6, 0, 5), (10, 2), (16, 0, 2), (10, 3), (16, 0, 3), (4, 1, 0),
+    (8, 0, 1, 0), (9, 1), (6, 0, 6), (4, 1, 1), (7, 0, 0), (16, 1, 1), (16, 1, 2), (4, 1, 2), (7, 0, 1), (10, 4),
+    (16, 0, 4), (4, 1, 3), (16, 1, 3), (7, 0, 2), (16, 1, 4), (4, 1, 4), (16, 1, 0), (15, 1, 0), (7, 0, 3), (4, 1, 5),
+    (7, 1, 0), (6, 0, 7), (4, 1, 6), (15, 1, 1), (7, 1, 1), (4, 1, 7), (15, 1, 2), (10, 5), (16, 0, 5), (16, 1, 5),
+    (15, 0, 1), (7, 1, 2), (15, 0, 0), (7, 1, 3), (7, 0, 4), (15, 0, 2), (7, 1, 4), (15, 1, 3), (10, 6), (16, 0, 6),
+    (16, 1, 6), (15, 0, 3), (10, 7), (8, 1, 1, 0), (8, 1, 1, 1), (7, 0, 5), (15, 1, 4), (7, 1, 5), (16, 0, 7),
+    (15, 0, 4), (16, 1, 7), (8, 1, 0, 0), (15, 1, 5), (8, 1, 1, 2), (8, 1, 0, 1), (15, 0, 5), (7, 0, 6), (7, 1, 6),
+    (15, 1, 6), (8, 1, 1, 3), (8, 1, 0, 3), (5, 2), (15, 0, 6), (8, 1, 1, 6), (8, 1, 0, 2), (7, 0, 7), (7, 1, 7),
+    (15, 1, 7), (8, 1, 1, 4), (6, 1, 0), (15, 0, 7), (8, 1, 0, 4), (8, 1, 1, 5), (8, 1, 0, 5), (8, 0, 2, 0), (9, 2),
+    (16, 2, 0), (15, 2, 0), (8, 1, 1, 7), (11, 0), (6, 1, 1), (16, 2, 4), (11, 4), (8, 1, 0, 6), (14, 1), (16, 2, 1),
+    (11, 1), (16, 2, 2), (11, 2), (8, 1, 0, 7), (16, 2, 3), (11, 3), (12, 0), (16, 2, 6), (7, 2, 0), (16, 2, 5),
+    (15, 2, 1), (14, 0), (11, 5), (13, 0), (16, 2, 7), (11, 6), (15, 2, 2), (8, 1, 2, 0), (11, 7), (6, 1, 2),
+    (17, 1, 0), (15, 2, 3), (7, 2, 1), (7, 2, 2), (12, 1), (7, 2, 3), (15, 2, 4), (6, 1, 3), (13, 1), (17, 1, 1),
+    (15, 2, 5), (15, 2, 6), (7, 2, 4), (7, 2, 5), (12, 2), (7, 2, 6), (13, 2), (17, 1, 2), (18, 0), (7, 2, 7),
+    (8, 1, 2, 1), (15, 2, 7), (6, 1, 4), (8, 1, 2, 2), (18, 1), (12, 3), (13, 3), (17, 1, 3), (8, 1, 2, 3),
+    (8, 1, 2, 4), (8, 1, 2, 5), (6, 1, 5), (8, 1, 2, 6), (8, 1, 2, 7), (14, 2), (17, 2, 0), (17, 2, 1), (17, 2, 2),
+    (6, 1, 6), (17, 2, 3), (18, 2), (6, 1, 7), (12, 4), (13, 4), (17, 2, 4), (17, 1, 4), (18, 3), (12, 5), (13, 5),
+    (17, 2, 5), (17, 1, 5), (12, 6), (13, 6), (17, 2, 6), (17, 1, 6), (18, 4), (12, 7), (13, 7), (17, 2, 7),
+    (17, 1, 7), (18, 5), (18, 6), (18, 7),
+)
+OUTER = (
+    (4, 0, 0), (0,), (4, 0, 1), (4, 0, 2), (4, 0, 3), (6, 0, 0), (10, 0), (6, 0, 1), (6, 0, 2), (4, 0, 4), (4, 0, 5),
+    (4, 0, 6), (10, 1), (4, 0, 7), (6, 0, 3), (5, 0), (2, 0), (1,), (2, 1), (3, 0), (3, 1), (9, 0), (16, 0, 0),
+    (11, 0), (16, 0, 1), (11, 1), (7, 0, 0), (10, 2), (7, 0, 1), (16, 0, 2), (6, 0, 4), (11, 2), (10, 3), (7, 0, 2),
+    (16, 0, 3), (6, 0, 5), (10, 4), (7, 0, 3), (16, 0, 4), (6, 0, 6), (11, 3), (7, 0, 6), (11, 4), (10, 5), (7, 0, 4),
+    (16, 0, 5), (7, 0, 5), (6, 0, 7), (11, 5), (10, 6), (16, 0, 6), (6, 1, 0), (11, 6), (10, 7), (4, 1, 0),
+    (16, 0, 7), (6, 1, 1), (7, 0, 7), (4, 1, 1), (4, 1, 2), (6, 1, 2), (4, 1, 3), (12, 0), (4, 1, 4), (13, 0),
+    (4, 1, 5), (6, 1, 3), (12, 1), (4, 1, 6), (6, 1, 4), (13, 1), (4, 1, 7), (12, 2), (6, 1, 5), (12, 3), (6, 1, 6),
+    (13, 2), (12, 4), (6, 1, 7), (13, 3), (12, 5), (12, 6), (11, 7), (13, 4), (15, 0, 0), (8, 1, 0, 0), (12, 7),
+    (13, 5), (15, 0, 1), (13, 6), (15, 0, 2), (8, 1, 0, 1), (15, 0, 3), (13, 7), (8, 1, 0, 3), (15, 0, 4), (15, 0, 5),
+    (8, 1, 0, 2), (8, 1, 0, 4), (15, 0, 6), (8, 1, 0, 5), (8, 1, 0, 6), (15, 0, 7), (8, 1, 0, 7), (14, 0), (18, 0),
+    (18, 1), (18, 2), (18, 3), (18, 4), (18, 5), (18, 6), (18, 7),
+)
 MESH = pl.DeviceIdType.MESH
 
 
@@ -289,12 +327,481 @@
                 pair(which, piece, shift).wait_send()
 
 
+def wide_kernel(
+    rows, cols, layers,
+    left_ref, middle_ref, right_ref, out_ref, stage,
+    a, b, part, cross, remote, pre, turned, far, fin,
+    a_local, turn_sem, a_send, a_recv, pre_sems, own_sems, load_sems, bz_sems, by_sems,
+    sx_sems, sc_sems, cross_sems, fwd_send, fwd_recv, o_send, o_recv, f_sems,
+):
+    group, side = rows // 2, cols // 2
+    z, col, y = lax.axis_index("row"), lax.axis_index("col"), lax.axis_index("layer")
+    x, c = col // side, lax.rem(col, side)
+    h, par = z // group, lax.rem(z, group)
+    straight = x == h
+    crossed = jnp.logical_not(straight)
+    inner = par != h
+    mate = h * group + 1 - par
+    near_z = (1 - h) * group + h
+    far_z = (1 - h) * group + 1 - h
+    depth = middle_ref.shape[0]
+    width = middle_ref.shape[1]
+    deep = left_ref.shape[1]
+    half = left_ref.shape[0] // layers
+    quarter = half // 2
+    w = width // PIECES
+    slabs = 3
+
+    def at(z_, x_, c_, y_):
+        return (z_, x_ * side + c_, y_)
+
+    greeted = []
+    for dx in range(2):
+        for dc in range(2):
+            for dy in range(2):
+                if dx or dc or dy:
+                    greeted.append(at(z, lax.rem(x + dx, 2), lax.rem(c + dc, 2), lax.rem(y + dy, 2)))
+    for dz in range(1, rows):
+        for dy in range(2):
+            greeted.append(at(lax.rem(z + dz, rows), x, c, lax.rem(y + dy, 2)))
+    barrier = pltpu.get_barrier_semaphore()
+    for device in greeted:
+        pl.semaphore_signal(barrier, inc=1, device_id=device, device_id_type=MESH)
+
+    def send(src, dst, send_sem, recv_sem, device):
+        return pltpu.make_async_remote_copy(
+            src_ref=src, dst_ref=dst, send_sem=send_sem, recv_sem=recv_sem,
+            device_id=device, device_id_type=MESH,
+        )
+
+    def when(flag, call, *args):
+        @pl.when(flag)
+        def _():
+            call(*args)
+
+    def left_rows(y_, s):
+        return left_ref.at[pl.ds(pl.multiple_of(y_ * half + s * quarter, quarter), quarter)]
+
+    def left_half(y_):
+        return left_ref.at[pl.ds(pl.multiple_of(y_ * half, half), half)]
+
+    def deep_cols(y_):
+        return pl.ds(pl.multiple_of(y_ * deep, deep), deep)
+
+    def rows_of(s):
+        return pl.ds(pl.multiple_of(s * quarter, quarter), quarter)
+
+    def a_piece(slab, s, y_):
+        return a.at[0, slab, c, rows_of(s), deep_cols(y_)]
+
+    def a_half(y_):
+        return a.at[0, 0, c, :, deep_cols(y_)]
+
+    there = jnp.where(inner, 1, 2)
+
+    def keep_left():
+        return pltpu.make_async_copy(left_half(y), a_half(y), a_local)
+
+    def turn_kept():
+        return send(left_half(1 - y), a_half(y), a_send.at[0], a_recv.at[0, y], at(z, x, c, 1 - y))
+
+    def turn_sent():
+        return send(left_half(1 - y), turned, a_send.at[0], turn_sem, at(z, x, c, 1 - y))
+
+    def side_left(k):
+        y_ = 1 - y if k else y
+        return send(a_half(y_) if k else left_half(y), a_half(y_), a_send.at[1 + k], a_recv.at[0, y_], at(z, 1 - x, c, y))
+
+    def give_left(k):
+        src = turned.at[rows_of(1 - x)] if k else left_rows(y, 1 - x)
+        return send(src, pre.at[k], a_send.at[1 + k], pre_sems.at[k], at(z, 1 - x, c, y))
+
+    def jump(src, k):
+        y_ = 1 - y if k else y
+        return send(src, a_piece(there, x, y_), a_send.at[3 + k], a_recv.at[there, y_], at(near_z, x, c, y))
+
+    def jump_left(k):
+        return jump(turned.at[rows_of(x)] if k else left_rows(y, x), k)
+
+    def left_start():
+        @pl.when(straight)
+        def _():
+            turn_kept().start()
+            side_left(0).start()
+            keep_left().start()
+
+        @pl.when(crossed)
+        def _():
+            turn_sent().start()
+            give_left(0).start()
+
+    def left_give():
+        @pl.when(crossed)
+        def _():
+            turn_sent().wait_recv()
+            give_left(1).start()
+
+    def left_jump(k):
+        @pl.when(crossed)
+        def _():
+            jump_left(k).start()
+
+    def left_relay(k):
+        @pl.when(straight)
+        def _():
+            give_left(k).wait_recv()
+            jump(pre.at[k], k).start()
+
+    def a_in(slab):
+        def arrived(y_):
+            ref = a_piece(slab, x, y_) if slab else a_half(y_)
+            send(ref, ref, a_send.at[0], a_recv.at[slab, y_], at(z, x, c, 1 - y)).wait_recv()
+
+        if slab:
+            arrived(0)
+            arrived(1)
+            spread_x(0, slab, 0, x).start()
+            spread_c(0, slab, 0, 0).start()
+        else:
+            @pl.when(straight)
+            def _():
+                arrived(1 - y)
+                side_left(1).start()
+                keep_left().wait()
+
+            @pl.when(crossed)
+            def _():
+                arrived(0)
+                arrived(1)
+
+            whole(0).start()
+
+    def a_block(phase, slab, s, n):
+        if phase:
+            return a.at[1, slab, c, rows_of(s), strip(n)]
+        return a.at[0, slab, c, rows_of(s)]
+
+    def spread_x(phase, slab, n, s):
+        ref = a_block(phase, slab, s, n)
+        k = n + phase
+        return send(ref, ref, sx_sems.at[slab, k, 0], sx_sems.at[slab, k, 1], at(z, 1 - x, c, y))
+
+    def spread_c(phase, slab, n, which):
+        ref = a_block(phase, slab, 1 - x if which else x, n)
+        k = n + phase
+        return send(ref, ref, sc_sems.at[slab, k, which, 0], sc_sems.at[slab, k, which, 1], at(z, x, 1 - c, y))
+
+    def whole(_):
+        ref = a.at[0, 0, c]
+        return send(ref, ref, sc_sems.at[0, 0, 0, 0], sc_sems.at[0, 0, 0, 1], at(z, x, 1 - c, y))
+
+    def pass_on(phase, slab, n):
+        spread_x(phase, slab, n, 1 - x).wait_recv()
+        spread_c(phase, slab, n, 1).start()
+
+    def a_ready(slab):
+        if slab:
+            for which in range(2):
+                spread_c(0, slab, 0, which).wait_recv()
+        else:
+            whole(0).wait_recv()
+
+    def a2_ready(slab):
+        for n in range(PIECES):
+            for which in range(2):
+                spread_c(1, slab, n, which).wait_recv()
+
+    sources = (middle_ref, right_ref)
+
+    def strip(n):
+        return pl.ds(n * w, w)
+
+    def b_rows(plane, y_):
+        return pl.ds(pl.multiple_of(plane * depth + y_ * (depth // 2), depth // 2), depth // 2)
+
+    def b_slot(phase, n, plane, y_):
+        if phase:
+            return stage.at[n, b_rows(0, y_)]
+        return b.at[n, b_rows(plane, y_)]
+
+    def bz(phase, n):
+        src = sources[phase].at[b_rows(0, y), strip(n)]
+        return send(src, b_slot(phase, n, par, y), bz_sems.at[phase, n, 0], bz_sems.at[phase, n, 1], at(mate, x, c, y))
+
+    def by(phase, n):
+        ref = b_slot(phase, n, 1 - par, y)
+        return send(ref, ref, by_sems.at[phase, n, 0], by_sems.at[phase, n, 1], at(z, x, c, 1 - y))
+
+    def own(phase, n):
+        rows_ = pl.ds(pl.multiple_of(par * depth, depth), depth)
+        return pltpu.make_async_copy(sources[phase].at[:, strip(n)], b.at[n, rows_], own_sems.at[phase, n])
+
+    def load(n):
+        rows_ = pl.ds(pl.multiple_of((1 - par) * depth, depth), depth)
+        return pltpu.make_async_copy(stage.at[n], b.at[n, rows_], load_sems.at[n])
+
+    def b_send(phase, n):
+        bz(phase, n).start()
+
+    def b_turn(phase, n):
+        bz(phase, n).wait_recv()
+        by(phase, n).start()
+
+    def b_ready(n):
+        own(0, n).wait()
+        by(0, n).wait_recv()
+
+    def b_own(n):
+        own(1, n).start()
+
+    def b_load(n):
+        by(0, n).wait_send()
+        by(1, n).wait_recv()
+        load(n).start()
+
+    def b_loaded(n):
+        own(1, n).wait()
+        load(n).wait()
+
+    def multiply(phase, slab, n, store):
+        def add(k, total):
+            deep_rows = pl.ds(pl.multiple_of(k * deep, deep), deep)
+            cols_ = pl.ds(pl.multiple_of(lax.rem(k, 2) * deep, deep), deep)
+            return total + jnp.dot(a[phase, slab, k // 2, :, cols_], b[n, deep_rows], preferred_element_type=jnp.float32)
+
+        store(n, lax.fori_loop(0, 2 * depth // deep, add, jnp.zeros((half, w), jnp.float32)))
+
+    def keep(slab):
+        def store(n, total):
+            part[slab, :, strip(n)] = total.astype(part.dtype)
+
+        return store
+
+    home_slab = (jnp.where(inner, 1, 2), 0, 0)
+    home_z = (near_z, near_z, far_z)
+
+    def cross_copy(slab, n):
+        return send(
+            part.at[slab, rows_of(1 - x), strip(n)], cross.at[slab, :, strip(n)],
+            cross_sems.at[slab, n, 0], cross_sems.at[slab, n, 1], at(z, 1 - x, c, y),
+        )
+
+    def fwd_copy(slab, n, src):
+        to = home_slab[slab]
+        return send(
+            src, remote.at[to, :, strip(n)], fwd_send.at[slab, n], fwd_recv.at[to, n],
+            at(home_z[slab], x, c, y),
+        )
+
+    def fwd_part(slab, n):
+        return fwd_copy(slab, n, part.at[slab, rows_of(x), strip(n)])
+
+    def fwd_cross(slab, n):
+        return fwd_copy(slab, n, cross.at[slab, :, strip(n)])
+
+    def unit1(slab, n):
+        multiply(0, slab, n, keep(slab))
+        cross_copy(slab, n).start()
+
+        @pl.when(crossed)
+        def _():
+            fwd_part(slab, n).start()
+
+    def relay1(slab, n):
+        @pl.when(straight)
+        def _():
+            cross_copy(slab, n).wait_recv()
+            fwd_cross(slab, n).start()
+
+    def reduce1(slab, n):
+        ref = remote.at[slab, :, strip(n)]
+        send(ref, ref, fwd_send.at[slab, n], fwd_recv.at[slab, n], at(z, x, c, 1 - y)).wait_recv()
+
+        def add(other, base):
+                @pl.loop(0, quarter // 32)
+                def _(i):
+                    span = pl.ds(pl.multiple_of(i * 32, 32), 32)
+                    into = pl.ds(pl.multiple_of(x * quarter + i * 32, 32), 32)
+                    mine = pl.ds(pl.multiple_of(base + i * 32, 32), 32)
+                    value = other[slab, mine, strip(n)].astype(jnp.float32) + remote[slab, span, strip(n)].astype(jnp.float32)
+                    a[1, slab, c, into, strip(n)] = value.astype(a.dtype)
+
+        @pl.when(straight)
+        def _():
+            add(part, x * quarter)
+
+        @pl.when(crossed)
+        def _():
+            cross_copy(slab, n).wait_recv()
+            add(cross, 0)
+
+        spread_x(1, slab, n, x).start()
+        spread_c(1, slab, n, 0).start()
+
+    def out_copy(slab, n):
+        return send(
+            part.at[slab, :, strip(n)], far.at[:, strip(n)], o_send.at[slab - 1, n], o_recv.at[n],
+            at(home_z[slab], x, c, y),
+        )
+
+    def unit2(slab, n):
+        cross_copy(slab, n).wait_send()
+        fwd_part(slab, n).wait_send()
+        multiply(1, slab, n, keep(slab))
+        out_copy(slab, n).start()
+
+    my_rows = pl.ds(pl.multiple_of(y * half, half), half)
+
+    def fin_copy(n):
+        cols_ = pl.ds(n % (PIECES // 2) * w, w)
+        return send(fin.at[n], out_ref.at[my_rows, cols_], f_sems.at[n, 0], f_sems.at[n, 1], at(z, x, c, 1 - y))
+
+    def unit3(n):
+        ref = far.at[:, strip(n)]
+        send(ref, ref, o_send.at[0, n], o_recv.at[n], at(z, x, c, 1 - y)).wait_recv()
+
+        def store(n, total):
+            value = total + far[:, strip(n)].astype(jnp.float32)
+            fin[n] = value.astype(fin.dtype)
+
+        multiply(1, 0, n, store)
+        mine = y == n // (PIECES // 2)
+
+        @pl.when(mine)
+        def _():
+            out_ref[my_rows, pl.ds(n % (PIECES // 2) * w, w)] = fin[n]
+
+        @pl.when(jnp.logical_not(mine))
+        def _():
+            fin_copy(n).start()
+
+    steps = (
+        left_start, left_give, left_jump, left_relay, b_send, a_in, b_turn, relay1, pass_on, a_ready,
+        b_ready, b_own, b_load, b_loaded, a2_ready, reduce1, unit1, unit2, unit3,
+    )
+    for n in range(PIECES):
+        own(0, n).start()
+    pl.semaphore_wait(barrier, len(greeted))
+
+    def follow(order):
+        for step, *args in order:
+            steps[step](*args)
+
+    when(inner, follow, INNER)
+    when(jnp.logical_not(inner), follow, OUTER)
+
+    for n in range(PIECES):
+        mine = y == n // (PIECES // 2)
+
+        @pl.when(mine)
+        def _():
+            fin_copy(n).wait_recv()
+
+        @pl.when(jnp.logical_not(mine))
+        def _():
+            fin_copy(n).wait_send()
+
+    @pl.when(straight)
+    def _():
+        turn_kept().wait_send()
+        for k in range(2):
+            side_left(k).wait_send()
+            jump(pre.at[k], k).wait_send()
+
+    @pl.when(crossed)
+    def _():
+        turn_sent().wait_send()
+        for k in range(2):
+            give_left(k).wait_send()
+            jump_left(k).wait_send()
+
+    for phase in range(2):
+        for n in range(PIECES):
+            bz(phase, n).wait_send()
+            if phase:
+                by(phase, n).wait_send()
+
+    def sent(slab):
+        if slab:
+            spread_x(0, slab, 0, x).wait_send()
+            for which in range(2):
+                spread_c(0, slab, 0, which).wait_send()
+        else:
+            whole(0).wait_send()
+        for n in range(PIECES):
+            spread_x(1, slab, n, x).wait_send()
+            for which in range(2):
+                spread_c(1, slab, n, which).wait_send()
+            if slab:
+                out_copy(slab, n).wait_send()
+            else:
+                cross_copy(slab, n).wait_send()
+                fwd_part(slab, n).wait_send()
+
+    sent(0)
+    for slab in range(1, slabs):
+        when(inner, sent, slab)
+
+
+def wide(rows, cols, layers, left, middle, right):
+    height, inner = left.shape
+    depth, width = middle.shape
+    half = height // layers
+    quarter = half // 2
+    bf16 = jnp.bfloat16
+    anywhere = pl.BlockSpec(memory_space=pl.ANY)
+    dma = pltpu.SemaphoreType.DMA
+    out, _ = pl.pallas_call(
+        functools.partial(wide_kernel, rows, cols, layers),
+        out_shape=(
+            jax.ShapeDtypeStruct((height, width // layers), bf16),
+            jax.ShapeDtypeStruct((PIECES, depth, width // PIECES), bf16),
+        ),
+        in_specs=[anywhere] * 3,
+        out_specs=(pl.BlockSpec(memory_space=pltpu.VMEM), anywhere),
+        scratch_shapes=[
+            pltpu.VMEM((2, 3, 2, half, depth), bf16),
+            pltpu.VMEM((PIECES, 2 * depth, width // PIECES), bf16),
+            pltpu.VMEM((3, half, width), bf16),
+            pltpu.VMEM((3, quarter, width), bf16),
+            pltpu.VMEM((3, quarter, width), bf16),
+            pltpu.VMEM((2, quarter, inner), bf16),
+            pltpu.VMEM((half, inner), bf16),
+            pltpu.VMEM((half, width), bf16),
+            pltpu.VMEM((PIECES, half, width // PIECES), bf16),
+            dma,
+            dma,
+            dma((5,)),
+            dma((3, 2)),
+            dma((2,)),
+            dma((2, PIECES)),
+            dma((PIECES,)),
+            dma((2, PIECES, 2)),
+            dma((2, PIECES, 2)),
+            dma((3, PIECES + 1, 2)),
+            dma((3, PIECES + 1, 2, 2)),
+            dma((3, PIECES, 2)),
+            dma((3, PIECES)),
+            dma((3, PIECES)),
+            dma((2, PIECES)),
+            dma((PIECES,)),
+            dma((PIECES, 2)),
+        ],
+        compiler_params=pltpu.CompilerParams(
+            collective_id=0, has_side_effects=True, vmem_limit_bytes=67043328
+        ),
+    )(left, middle, right)
+    return out
+
+
 def per_device(left, middle, right):
     rows, cols, layers = (lax.axis_size(name) for name in ("row", "col", "layer"))
     height, inner = left.shape
     width = right.shape[1] // layers
     depth = right.shape[0]
     group = rows // 2
+    if (rows, cols, layers) == (2 * PAIR, 2 * PAIR, PAIR) and depth == layers * inner:
+        return wide(rows, cols, layers, left, middle, right)
     partners = cols // 2 * layers - 1
     bf16 = jnp.bfloat16
     anywhere = pl.BlockSpec(memory_space=pl.ANY)

time: 409 us -> 369 us (0.902); the launches traced: 403 us -> 369 us
  Pallas kernels: 400 us -> 366 us
    pallas_call x1, Pallas kernels: 400 us -> 366 us  [wide(): pl.pallas_call(functools.partial(wide_kernel, rows, cols, layers), out_sh...]
where the time goes in v1:
time: 369 us
  Pallas kernels  366 us (99%)
    pallas_call x1, Pallas kernels, wide(): pl.pallas_call(functools.partial(wide_kernel, rows, cols, layers), out_sh...  366 us

profile of v1, /device:TPU:14, one launch (start us, length us, event | category | flops | bytes accessed | tf_op | source)
XLA Modules:
  0.0 369.1 jit_solution(5331041208076481173)
XLA Ops:
  0.0 366.0 %shard_map.37 = (bf16[1024,1024]{1,0:T(8,128)(2,1)}, bf16[8,2048,256]{2,1,0:T(8,128)(2,1)}) custom-call(bf16[1024,1024]{1,0:T(8,128)(2,1)} %left_ref.1, bf16[2048,2048]{1,0:T(8,128)(2,1)} %middle_ref.1, bf16[2048,2048]{1,0:T(8,128)(2,1)} %right_ref.1), custom_call_target="tpu_custom_call" | custom-call | tf_op jit(solution)/shard_map/pallas_call | solution.py:754
  366.0 3.1 copy.5

commit v2 on v1

--- a/solution.py
+++ b/solution.py
@@ -17,8 +17,8 @@
     (3, 1), (5, 1), (6, 0, 4), (16, 0, 0), (6, 0, 5), (10, 2), (16, 0, 2), (10, 3), (16, 0, 3), (4, 1, 0),
     (8, 0, 1, 0), (9, 1), (6, 0, 6), (4, 1, 1), (7, 0, 0), (16, 1, 1), (16, 1, 2), (4, 1, 2), (7, 0, 1), (10, 4),
     (16, 0, 4), (4, 1, 3), (16, 1, 3), (7, 0, 2), (16, 1, 4), (4, 1, 4), (16, 1, 0), (15, 1, 0), (7, 0, 3), (4, 1, 5),
-    (7, 1, 0), (6, 0, 7), (4, 1, 6), (15, 1, 1), (7, 1, 1), (4, 1, 7), (15, 1, 2), (10, 5), (16, 0, 5), (16, 1, 5),
-    (15, 0, 1), (7, 1, 2), (15, 0, 0), (7, 1, 3), (7, 0, 4), (15, 0, 2), (7, 1, 4), (15, 1, 3), (10, 6), (16, 0, 6),
+    (7, 1, 0), (6, 0, 7), (4, 1, 6), (15, 1, 1), (7, 1, 1), (4, 1, 7), (15, 1, 3), (15, 1, 2), (10, 5), (16, 0, 5),
+    (16, 1, 5), (15, 0, 1), (7, 1, 2), (15, 0, 0), (7, 1, 3), (7, 0, 4), (15, 0, 2), (7, 1, 4), (10, 6), (16, 0, 6),
     (16, 1, 6), (15, 0, 3), (10, 7), (8, 1, 1, 0), (8, 1, 1, 1), (7, 0, 5), (15, 1, 4), (7, 1, 5), (16, 0, 7),
     (15, 0, 4), (16, 1, 7), (8, 1, 0, 0), (15, 1, 5), (8, 1, 1, 2), (8, 1, 0, 1), (15, 0, 5), (7, 0, 6), (7, 1, 6),
     (15, 1, 6), (8, 1, 1, 3), (8, 1, 0, 3), (5, 2), (15, 0, 6), (8, 1, 1, 6), (8, 1, 0, 2), (7, 0, 7), (7, 1, 7),

time: 369 us -> 372 us (level)
  no operation moved by 1% of the time
where the time goes in v2:
time: 372 us
  Pallas kernels  369 us (99%)
    pallas_call x1, Pallas kernels, wide(): pl.pallas_call(functools.partial(wide_kernel, rows, cols, layers), out_sh...  369 us

profile of v2, /device:TPU:14, one launch (start us, length us, event | category | flops | bytes accessed | tf_op | source)
XLA Modules:
  0.0 371.9 jit_solution(654218374521767715)
XLA Ops:
  0.0 368.8 %shard_map.37 = (bf16[1024,1024]{1,0:T(8,128)(2,1)}, bf16[8,2048,256]{2,1,0:T(8,128)(2,1)}) custom-call(bf16[1024,1024]{1,0:T(8,128)(2,1)} %left_ref.1, bf16[2048,2048]{1,0:T(8,128)(2,1)} %middle_ref.1, bf16[2048,2048]{1,0:T(8,128)(2,1)} %right_ref.1), custom_call_target="tpu_custom_call" | custom-call | tf_op jit(solution)/shard_map/pallas_call | solution.py:754
  368.8 3.1 copy.5
